TPU v7x, 32 devices: a whole 2x2x4 slice. The times are simulated.
32 devices in a mesh: groups: 2 (over x), seq: 16 (over z, y, core).
Axes of the slice: x: 2, y: 2, z: 4, core: 2. Of those that a mesh axis runs over, the one named last changes fastest.
Arguments:
- queries: bfloat16 [8192, 4096], P(('groups', 'seq')), parts along dimension 0, may hold values from -13 to 13
- keys: bfloat16 [8192, 512], P(('groups', 'seq')), parts along dimension 0, may hold values from -13 to 13
- values: bfloat16 [8192, 512], P(('groups', 'seq')), parts along dimension 0, may hold values from -6 to 6
- segment_ids: int32 [8192], P(('groups', 'seq')), parts along dimension 0, may hold values from 0 to 8, as said below
Outputs:
- attended: bfloat16 [8192, 4096], P(('groups', 'seq')), parts along dimension 0
- rotated_keys: bfloat16 [8192, 512], P(('groups', 'seq')), parts along dimension 0
There are 2 independent parts, one for each index of `groups`. A program takes and returns all parts, laid end to end along the dimension named above; each array names one. Nothing has to cross between parts.
Inputs may be any that keep to these rules, and one draw needn't show every extreme that they name: `segment_ids`: never falling along the packed stream, starting at 0 and rising by one at each new rollout; each rollout covers 1 to 1792 tokens and one covers exactly 1792.
All inputs are finite; a program needn't handle non-finite values.
Results may differ from a plain program's by a relative error of at most 0.0054.
Values may be sent and summed in bfloat16 or wider, within the bound.
A program may use at most 192 MiB of HBM per device.

v0:
```python
from functools import partial

import jax
import jax.numpy as jnp
from jax import lax
from jax.experimental import pallas as pl
from jax.experimental.pallas import tpu as pltpu
from jax.sharding import PartitionSpec as P

HD = 128
SPAN = 7
ROPE_BASE = 1000000.0
BIG = 1e30
NO_SEGMENT = 127
LANES = 128
ONES_ROWS = 16


def shifted(shard, axis, by):
    length = lax.axis_size(axis)
    pairs = [(i, i + by) for i in range(length) if 0 <= i + by < length]
    return lax.ppermute(shard, axis, pairs)


def tables(positions):
    half_dim = HD // 2
    inverse_freq = ROPE_BASE ** (-(jnp.arange(half_dim, dtype=jnp.float32) * (2.0 / HD)))
    angles = positions.astype(jnp.float32)[:, None] * inverse_freq[None, :]
    cosine, sine = jnp.cos(angles), jnp.sin(angles)
    return (
        jnp.concatenate([cosine, cosine], axis=-1),
        jnp.concatenate([-sine, sine], axis=-1),
    )


def rotate_heads(matrix, cosine, sine):
    rows, width = matrix.shape
    heads = matrix.astype(jnp.float32).reshape(rows, width // HD, HD)
    swapped = jnp.concatenate([heads[..., HD // 2 :], heads[..., : HD // 2]], axis=-1)
    turned = heads * cosine[:, None, :] + swapped * sine[:, None, :]
    return turned.reshape(rows, width).astype(jnp.bfloat16)


def one_hot(segment_row):
    rows = lax.broadcasted_iota(jnp.int32, (LANES, segment_row.shape[1]), 0)
    return jnp.where(rows == segment_row, 1.0, 0.0).T


def attend_phase(slots, head, group, qa, qhot, k_ref, khot, vt, top, acc, causal):
    first = causal is not None
    query = jnp.concatenate([qa[head], qhot[...]], axis=1)
    kv = head // group
    columns = pl.ds(pl.multiple_of(kv * HD, HD), HD)
    parts = []
    for slot in slots:
        key = jnp.concatenate([k_ref[slot, :, columns], khot[slot]], axis=1)
        part = lax.dot_general(
            key, query, (((1,), (1,)), ((), ())), preferred_element_type=jnp.float32
        )
        parts.append(part + causal[...] if first else part)
    new_top = jnp.max(parts[0], axis=0, keepdims=True)
    for part in parts[1:]:
        new_top = jnp.maximum(new_top, jnp.max(part, axis=0, keepdims=True))
    if not first:
        old_top = top[head]
        new_top = jnp.maximum(new_top, old_top)
    mixed = None
    for slot, part in zip(slots, parts):
        weights = jnp.exp2(part - new_top).astype(jnp.bfloat16)
        term = jnp.dot(vt[slot, kv], weights, preferred_element_type=jnp.float32)
        mixed = term if mixed is None else mixed + term
    if not first:
        mixed = mixed + acc[head] * jnp.exp2(old_top - new_top)
    return new_top, mixed


def kernel(
    group, phases, q_ref, cos_ref, sin_ref, k_ref, v_ref, seg_ref, out_ref,
    qa, qhot, khot, vt, top, acc, causal,
):
    rows = q_ref.shape[0]
    heads = q_ref.shape[1] // HD
    kv_heads = heads // group
    count = k_ref.shape[0]
    scale = HD ** (-0.5) * 1.4426950408889634
    cosine = cos_ref[...] * scale
    sine = sin_ref[...] * scale

    def turn(head, carry):
        columns = pl.ds(pl.multiple_of(head * HD, HD), HD)
        x = q_ref[:, columns].astype(jnp.float32)
        qa[head] = (x * cosine + pltpu.roll(x, HD // 2, 1) * sine).astype(jnp.bfloat16)
        return carry

    lax.fori_loop(0, heads, turn, 0)
    qhot[...] = ((one_hot(seg_ref[0]) - 1.0) * BIG).astype(jnp.bfloat16)
    key_at = lax.broadcasted_iota(jnp.int32, (rows, rows), 0)
    query_at = lax.broadcasted_iota(jnp.int32, (rows, rows), 1)
    causal[...] = jnp.where(key_at <= query_at, 0.0, -BIG)

    def prepare(slot, carry):
        khot[slot] = one_hot(seg_ref[slot]).astype(jnp.bfloat16)
        for kv in range(kv_heads):
            vt[slot, kv, :HD, :] = (
                v_ref[slot, :, kv * HD : (kv + 1) * HD].astype(jnp.float32).T.astype(jnp.bfloat16)
            )
            vt[slot, kv, HD:, :] = jnp.ones((ONES_ROWS, rows), jnp.bfloat16)
        return carry

    lax.fori_loop(0, count, prepare, 0)
    for number, slots in enumerate(phases):
        last = number == len(phases) - 1

        def step(index, carry):
            for head in (2 * index, 2 * index + 1):
                new_top, mixed = attend_phase(
                    slots, head, group, qa, qhot, k_ref, khot, vt, top, acc,
                    causal if number == 0 else None,
                )
                if last:
                    columns = pl.ds(pl.multiple_of(head * HD, HD), HD)
                    result = mixed[:HD] * (1.0 / mixed[HD : HD + 1])
                    out_ref[:, columns] = result.T.astype(jnp.bfloat16)
                else:
                    top[head] = new_top
                    acc[head] = mixed
            return carry

        lax.fori_loop(0, heads // 2, step, 0)


def local(queries, keys, values, segment_ids):
    block_rows = queries.shape[0]
    query_heads = queries.shape[1] // HD
    kv_heads = keys.shape[1] // HD
    group = query_heads // kv_heads
    my_rank = lax.axis_index("seq")
    row_index = my_rank * block_rows + jnp.arange(block_rows, dtype=jnp.int32)
    cosine, sine = tables(row_index)
    key_stack = rotate_heads(keys, cosine, sine)[None]
    value_stack = values[None]
    seg_stack = segment_ids[None, None]
    for stride_bit in range((SPAN + 1).bit_length() - 1):
        far = shifted((key_stack, value_stack, seg_stack), "seq", 1 << stride_bit)
        key_stack = jnp.concatenate([key_stack, far[0]], axis=0)
        value_stack = jnp.concatenate([value_stack, far[1]], axis=0)
        seg_stack = jnp.concatenate([seg_stack, far[2]], axis=0)
    count = key_stack.shape[0]
    present = jnp.arange(count) <= my_rank
    seg_stack = jnp.where(present[:, None, None], seg_stack, NO_SEGMENT)
    vmem = pl.BlockSpec(memory_space=pltpu.VMEM)
    attended = pl.pallas_call(
        partial(kernel, group, ((0,), (1, 2, 3, 4), (5, 6, 7))),
        out_shape=jax.ShapeDtypeStruct(queries.shape, jnp.bfloat16),
        in_specs=[vmem] * 6,
        out_specs=vmem,
        scratch_shapes=[
            pltpu.VMEM((query_heads, block_rows, HD), jnp.bfloat16),
            pltpu.VMEM((block_rows, LANES), jnp.bfloat16),
            pltpu.VMEM((count, block_rows, LANES), jnp.bfloat16),
            pltpu.VMEM((count, kv_heads, HD + ONES_ROWS, block_rows), jnp.bfloat16),
            pltpu.VMEM((query_heads, 1, block_rows), jnp.float32),
            pltpu.VMEM((query_heads, HD + ONES_ROWS, block_rows), jnp.float32),
            pltpu.VMEM((block_rows, block_rows), jnp.float32),
        ],
        compiler_params=pltpu.CompilerParams(vmem_limit_bytes=60 * 1024 * 1024),
    )(queries, cosine, sine, key_stack, value_stack, seg_stack)

    boundary = jnp.concatenate(
        [jnp.ones((1,), dtype=jnp.bool_), segment_ids[1:] != segment_ids[:-1]]
    )
    local_start = lax.cummax(jnp.where(boundary, row_index, -1), axis=0)
    earlier = jnp.sum((seg_stack[1:] == segment_ids[0]).astype(jnp.int32))
    starts = jnp.where(
        segment_ids == segment_ids[0], my_rank * block_rows - earlier, local_start
    )
    turned_keys = rotate_heads(keys, *tables(row_index - starts))
    return (attended, turned_keys)


def solution(mesh):
    in_specs = (
        P(("groups", "seq"), None),
        P(("groups", "seq"), None),
        P(("groups", "seq"), None),
        P(("groups", "seq")),
    )
    out_specs = (P(("groups", "seq"), None), P(("groups", "seq"), None))
    return jax.shard_map(local, mesh=mesh, in_specs=in_specs, out_specs=out_specs, check_vma=False)
```

profile of v0, /device:TPU:29, one launch (start us, length us, event | category | flops | bytes accessed | tf_op | source)
XLA Modules:
  0.0 166.9 jit_solution(7086196797809766245)
XLA Ops:
  0.6 0.0 copy-start.5
  0.6 1.3 collective-permute-start.6
  1.9 1.3 collective-permute-start.3
  3.2 0.8 slice_compare_fusion
  4.1 0.1 fusion.6
  4.2 0.3 reduce-window.9
  4.5 0.1 slice.34
  4.6 1.1 reshape.131
  5.7 0.3 fusion.10
  6.0 0.1 slice_reduce_fusion
  6.1 0.0 collective-permute-done.6
  6.2 0.0 copy-done.5
  6.2 1.3 collective-permute-start.7
  7.5 4.8 %collective-permute-done.7 = s32[2,1,256]{2,1,0:T(1,128)S(1)} collective-permute-done((s32[2,1,256]{2,1,0:T(1,128)S(1)}, s32[2,1,256]{2,1,0:T(1,128)S(1)}, u32[]{:S(2)}, u32[]{:S(2)}) %collective-permute-start.7) | collective-permute-done | bytes 2080 | tf_op jit(solution)/shard_map/ppermute | solution.py:22
  12.3 1.3 collective-permute-start.8
  13.6 0.5 slice.30
  14.1 2.5 %collective-permute-done.8 = s32[4,1,256]{2,1,0:T(1,128)S(1)} collective-permute-done((s32[4,1,256]{2,1,0:T(1,128)S(1)}, s32[4,1,256]{2,1,0:T(1,128)S(1)}, u32[]{:S(2)}, u32[]{:S(2)}) %collective-permute-start.8) | collective-permute-done | bytes 4128 | tf_op jit(solution)/shard_map/ppermute | solution.py:22
  16.7 0.1 broadcast_select_fusion.seg_ref
  16.7 0.0 copy-start.4
  16.7 1.3 fusion.5
  18.7 0.7 fusion.8
  19.4 1.0 multiply_cosine_fusion
  20.4 0.1 pad_maximum_fusion.9
  20.5 0.1 pad_maximum_fusion.7.cos_ref
  20.6 0.0 copy-start.2
  20.6 0.1 pad_maximum_fusion.8.sin_ref
  20.7 0.0 copy-start.1
  20.8 0.0 copy-start.3
  20.8 0.1 pad_maximum_fusion.10
  20.9 0.4 broadcast_multiply_fusion
  21.3 0.0 copy-done.4
  21.3 0.0 copy-start
  21.3 0.1 mul.99
  21.4 0.1 mul.91
  21.5 0.0 copy-done.2
  21.5 0.2 copy-done.3
  21.8 1.0 fusion
  22.7 0.0 copy-done.1
  22.7 1.3 collective-permute-start
  24.0 0.0 collective-permute-done.3
  24.0 0.0 copy-done
  24.1 0.1 pad_maximum_fusion.6
  24.1 1.3 collective-permute-start.4
  25.4 2.8 %collective-permute-done = bf16[1,256,512]{2,1,0:T(8,128)(2,1)S(1)} collective-permute-done((bf16[1,256,512]{2,1,0:T(8,128)(2,1)S(1)}, bf16[1,256,512]{2,1,0:T(8,128)(2,1)S(1)}, u32[]{:S(2)}, u32[]{:S(2)}) %collective-permute-start) | collective-permute-done | bytes 262176 | tf_op jit(solution)/shard_map/ppermute | solution.py:22
  28.2 0.1 pad_maximum_fusion.5
  28.2 1.3 collective-permute-start.1
  29.5 13.6 %collective-permute-done.4 = bf16[2,256,512]{2,1,0:T(8,128)(2,1)S(1)} collective-permute-done((bf16[2,256,512]{2,1,0:T(8,128)(2,1)S(1)}, bf16[2,256,512]{2,1,0:T(8,128)(2,1)S(1)}, u32[]{:S(2)}, u32[]{:S(2)}) %collective-permute-start.4) | collective-permute-done | bytes 524320 | tf_op jit(solution)/shard_map/ppermute | solution.py:22
  43.1 0.1 pad_maximum_fusion.3
  43.2 1.3 collective-permute-start.5
  44.5 9.8 %collective-permute-done.1 = bf16[2,256,512]{2,1,0:T(8,128)(2,1)S(1)} collective-permute-done((bf16[2,256,512]{2,1,0:T(8,128)(2,1)S(1)}, bf16[2,256,512]{2,1,0:T(8,128)(2,1)S(1)}, u32[]{:S(2)}, u32[]{:S(2)}) %collective-permute-start.1) | collective-permute-done | bytes 524320 | tf_op jit(solution)/shard_map/ppermute | solution.py:22
  54.3 0.1 pad_maximum_fusion.2
  54.5 1.3 collective-permute-start.2
  55.8 24.3 %collective-permute-done.5 = bf16[4,256,512]{2,1,0:T(8,128)(2,1)S(1)} collective-permute-done((bf16[4,256,512]{2,1,0:T(8,128)(2,1)S(1)}, bf16[4,256,512]{2,1,0:T(8,128)(2,1)S(1)}, u32[]{:S(2)}, u32[]{:S(2)}) %collective-permute-start.5) | collective-permute-done | bytes 1048608 | tf_op jit(solution)/shard_map/ppermute | solution.py:22
  80.1 1.5 pad_maximum_fusion.1.v_ref
  81.6 20.5 %collective-permute-done.2 = bf16[4,256,512]{2,1,0:T(8,128)(2,1)S(1)} collective-permute-done((bf16[4,256,512]{2,1,0:T(8,128)(2,1)S(1)}, bf16[4,256,512]{2,1,0:T(8,128)(2,1)S(1)}, u32[]{:S(2)}, u32[]{:S(2)}) %collective-permute-start.2) | collective-permute-done | bytes 1048608 | tf_op jit(solution)/shard_map/ppermute | solution.py:22
  102.1 1.5 pad_maximum_fusion.k_ref
  103.6 63.3 %shard_map.59 = bf16[256,4096]{1,0:T(8,128)(2,1)} custom-call(bf16[256,4096]{1,0:T(8,128)(2,1)} %q_ref.1, f32[256,128]{1,0:T(8,128)} %copy-done.2, f32[256,128]{1,0:T(8,128)} %copy-done.1, bf16[8,256,512]{2,1,0:T(8,128)(2,1)} %pad_maximum_fusion.k_ref, bf16[8,256,512]{2,1,0:T(8,128)(2,1)} %pad_maximum_fusion.1.v_ref, s32[8,1,256]{2,1,0:T(1,128)} %copy-done.4), custom_call_target="tpu_custom_call" | custom-call | tf_op jit(solution)/shard_map/pallas_call | solution.py:152
  (5 shorter events, 0.1 us)
Async XLA Ops:
  0.6 5.5 %copy-start.5 = (s32[256]{0:T(256)S(1)}, s32[256]{0:T(256)}, u32[]{:S(2)}) copy-start(s32[256]{0:T(256)} %param.7) | copy-start | bytes 3076
  0.6 5.5 %collective-permute-start.6 = (s32[1,1,256]{2,1,0:T(1,128)}, s32[1,1,256]{2,1,0:T(1,128)S(1)}, u32[]{:S(2)}, u32[]{:S(2)}) collective-permute-start(s32[1,1,256]{2,1,0:T(1,128)} %bitcast.43), channel_id=1, source_target_pairs={{0,1},{1,2},{2,3},{3,4},{4,5},{5,6},{6,7},{7,8},{8,9},{9,10},{10,1... | collective-permute-start | bytes 3080 | tf_op jit(solution)/shard_map/ppermute | solution.py:22
  1.9 22.1 %collective-permute-start.3 = (bf16[1,256,512]{2,1,0:T(8,128)(2,1)}, bf16[1,256,512]{2,1,0:T(8,128)(2,1)S(1)}, u32[]{:S(2)}, u32[]{:S(2)}) collective-permute-start(bf16[1,256,512]{2,1,0:T(8,128)(2,1)} %bitcast.35), channel_id=1, source_target_pairs={{0,1},{1,2},{2,3},{3,4},{4,5},{5,6},{6,7},{7,8},{8,9},{9,10},{10,1... | collective-permute-start | bytes 786440 | tf_op jit(solution)/shard_map/ppermute | solution.py:22
  6.2 6.1 %collective-permute-start.7 = (s32[2,1,256]{2,1,0:T(1,128)S(1)}, s32[2,1,256]{2,1,0:T(1,128)S(1)}, u32[]{:S(2)}, u32[]{:S(2)}) collective-permute-start(s32[2,1,256]{2,1,0:T(1,128)S(1)} %pad_add_fusion.1), channel_id=1, source_target_pairs={{0,2},{1,3},{2,4},{3,5},{4,6},{5,7},{6,8},{7,9},{8,10},{9,11},{10,... | collective-permute-start | bytes 6152 | tf_op jit(solution)/shard_map/ppermute | solution.py:22
  12.3 4.3 %collective-permute-start.8 = (s32[4,1,256]{2,1,0:T(1,128)S(1)}, s32[4,1,256]{2,1,0:T(1,128)S(1)}, u32[]{:S(2)}, u32[]{:S(2)}) collective-permute-start(s32[4,1,256]{2,1,0:T(1,128)S(1)} %pad_add_fusion), channel_id=1, source_target_pairs={{0,4},{1,5},{2,6},{3,7},{4,8},{5,9},{6,10},{7,11},{8,12},{9,13},{1... | collective-permute-start | bytes 12296 | tf_op jit(solution)/shard_map/ppermute | solution.py:22
  16.7 4.6 %copy-start.4 = (s32[8,1,256]{2,1,0:T(1,128)}, s32[8,1,256]{2,1,0:T(1,128)S(1)}, u32[]{:S(2)}) copy-start(s32[8,1,256]{2,1,0:T(1,128)S(1)} %broadcast_select_fusion.seg_ref) | copy-start | bytes 24580
  20.6 0.9 copy-start.2
  20.7 2.0 %copy-start.1 = (f32[256,128]{1,0:T(8,128)}, f32[256,128]{1,0:T(8,128)S(1)}, u32[]{:S(2)}) copy-start(f32[256,128]{1,0:T(8,128)S(1)} %pad_maximum_fusion.8.sin_ref) | copy-start | bytes 393220
  20.8 1.0 copy-start.3
  21.3 2.7 %copy-start = (bf16[256,512]{1,0:T(8,128)(2,1)S(1)}, bf16[256,512]{1,0:T(8,128)(2,1)}, u32[]{:S(2)}) copy-start(bf16[256,512]{1,0:T(8,128)(2,1)} %param.6) | copy-start | bytes 786436
  22.7 5.4 %collective-permute-start = (bf16[1,256,512]{2,1,0:T(8,128)(2,1)S(1)}, bf16[1,256,512]{2,1,0:T(8,128)(2,1)S(1)}, u32[]{:S(2)}, u32[]{:S(2)}) collective-permute-start(bf16[1,256,512]{2,1,0:T(8,128)(2,1)S(1)} %get-tuple-element.7), channel_id=1, source_target_pairs={{0,1},{1,2},{2,3},{3,4},{4,5},{5,6},{6,7},{7,8},{8,9},{9,10},{10,1... | collective-permute-start | bytes 786440 | tf_op jit(solution)/shard_map/ppermute | solution.py:22
  24.1 19.0 %collective-permute-start.4 = (bf16[2,256,512]{2,1,0:T(8,128)(2,1)S(1)}, bf16[2,256,512]{2,1,0:T(8,128)(2,1)S(1)}, u32[]{:S(2)}, u32[]{:S(2)}) collective-permute-start(bf16[2,256,512]{2,1,0:T(8,128)(2,1)S(1)} %pad_maximum_fusion.6), channel_id=1, source_target_pairs={{0,2},{1,3},{2,4},{3,5},{4,6},{5,7},{6,8},{7,9},{8,10},{9,11},{10,... | collective-permute-start | bytes 1572872 | tf_op jit(solution)/shard_map/ppermute | solution.py:22
  28.2 26.1 %collective-permute-start.1 = (bf16[2,256,512]{2,1,0:T(8,128)(2,1)S(1)}, bf16[2,256,512]{2,1,0:T(8,128)(2,1)S(1)}, u32[]{:S(2)}, u32[]{:S(2)}) collective-permute-start(bf16[2,256,512]{2,1,0:T(8,128)(2,1)S(1)} %pad_maximum_fusion.5), channel_id=1, source_target_pairs={{0,2},{1,3},{2,4},{3,5},{4,6},{5,7},{6,8},{7,9},{8,10},{9,11},{10,... | collective-permute-start | bytes 1572872 | tf_op jit(solution)/shard_map/ppermute | solution.py:22
  43.2 36.8 %collective-permute-start.5 = (bf16[4,256,512]{2,1,0:T(8,128)(2,1)S(1)}, bf16[4,256,512]{2,1,0:T(8,128)(2,1)S(1)}, u32[]{:S(2)}, u32[]{:S(2)}) collective-permute-start(bf16[4,256,512]{2,1,0:T(8,128)(2,1)S(1)} %pad_maximum_fusion.3), channel_id=1, source_target_pairs={{0,4},{1,5},{2,6},{3,7},{4,8},{5,9},{6,10},{7,11},{8,12},{9,13},{1... | collective-permute-start | bytes 3145736 | tf_op jit(solution)/shard_map/ppermute | solution.py:22
  54.5 47.6 %collective-permute-start.2 = (bf16[4,256,512]{2,1,0:T(8,128)(2,1)S(1)}, bf16[4,256,512]{2,1,0:T(8,128)(2,1)S(1)}, u32[]{:S(2)}, u32[]{:S(2)}) collective-permute-start(bf16[4,256,512]{2,1,0:T(8,128)(2,1)S(1)} %pad_maximum_fusion.2), channel_id=1, source_target_pairs={{0,4},{1,5},{2,6},{3,7},{4,8},{5,9},{6,10},{7,11},{8,12},{9,13},{1... | collective-permute-start | bytes 3145736 | tf_op jit(solution)/shard_map/ppermute | solution.py:22
where the time goes:
time: 167 us
  waiting for transfers between devices  78.3 us (47%)
  Pallas kernels  63.3 us (38%)
  starting transfers between devices  11.6 us (7%)
  other arithmetic  9.53 us (6%)
  local copies, waits for them, and re-layouts  2.59 us (2%)
    ppermute x9, waiting for transfers between devices, shifted(): return lax.ppermute(shard, axis, pairs)  78.3 us
    pallas_call x1, Pallas kernels, local(): pl.pallas_call(partial(kernel, group, ((0,), (1, 2, 3, 4), (5, 6, 7))), o...  63.3 us
    ppermute x9, starting transfers between devices, shifted(): return lax.ppermute(shard, axis, pairs)  11.6 us
  transfers between devices with their start and end apart: 9, of which 7 were waited for; matrix products, arithmetic and copies ran while one was open for 6% of the time, Pallas kernels for 0%

commit v1 on v0

v1 whole, which is shorter than its diff:
```python
from functools import partial

import jax
import jax.numpy as jnp
from jax import lax
from jax.experimental import pallas as pl
from jax.experimental.pallas import tpu as pltpu
from jax.sharding import PartitionSpec as P

HD = 128
SPAN = 7
ROPE_BASE = 1000000.0
BIG = 1e30
NO_SEGMENT = 127
LANES = 128
ONES_ROWS = 16
SEG_ROWS = 16
PIECES = 4


def tables(positions):
    half_dim = HD // 2
    inverse_freq = ROPE_BASE ** (-(jnp.arange(half_dim, dtype=jnp.float32) * (2.0 / HD)))
    angles = positions.astype(jnp.float32)[:, None] * inverse_freq[None, :]
    cosine, sine = jnp.cos(angles), jnp.sin(angles)
    return (
        jnp.concatenate([cosine, cosine], axis=-1),
        jnp.concatenate([-sine, sine], axis=-1),
    )


def rotate_heads(matrix, cosine, sine):
    rows, width = matrix.shape
    heads = matrix.astype(jnp.float32).reshape(rows, width // HD, HD)
    swapped = jnp.concatenate([heads[..., HD // 2 :], heads[..., : HD // 2]], axis=-1)
    turned = heads * cosine[:, None, :] + swapped * sine[:, None, :]
    return turned.reshape(rows, width).astype(jnp.bfloat16)


def one_hot(segment_row):
    rows = lax.broadcasted_iota(jnp.int32, (LANES, segment_row.shape[1]), 0).astype(jnp.float32)
    return jnp.where(rows == segment_row, 1.0, 0.0).T


def attend_phase(slots, head, group, qa, qhot, block, khot, vt, top, acc, causal):
    first = causal is not None
    rows = qhot.shape[0]
    query = jnp.concatenate([qa[head], qhot[...]], axis=1)
    kv = head // group
    at = pl.ds(pl.multiple_of(SEG_ROWS + kv * rows, SEG_ROWS), rows)
    parts = []
    for slot in slots:
        key = jnp.concatenate([block(slot)[at, :HD], khot[slot]], axis=1)
        part = lax.dot_general(
            key, query, (((1,), (1,)), ((), ())), preferred_element_type=jnp.float32
        )
        parts.append(part + causal[...] if first else part)
    new_top = jnp.max(parts[0], axis=0, keepdims=True)
    for part in parts[1:]:
        new_top = jnp.maximum(new_top, jnp.max(part, axis=0, keepdims=True))
    if not first:
        old_top = top[head]
        new_top = jnp.maximum(new_top, old_top)
    mixed = None
    for slot, part in zip(slots, parts):
        weights = jnp.exp2(part - new_top).astype(jnp.bfloat16)
        term = jnp.dot(vt[slot, kv], weights, preferred_element_type=jnp.float32)
        mixed = term if mixed is None else mixed + term
    if not first:
        mixed = mixed + acc[head] * jnp.exp2(old_top - new_top)
    return new_top, mixed


def kernel(
    group, count, q_ref, cos_ref, sin_ref, own_ref, keys_ref, freq_ref, out_ref, rot_ref,
    recv, qa, qhot, khot, vt, top, acc, causal, send_sems, recv_sems,
):
    rows = q_ref.shape[0]
    heads = q_ref.shape[1] // HD
    kv_heads = heads // group
    me = lax.axis_index("seq")
    core = lax.rem(me, 2)
    side = lax.rem(me // 2, 2)
    plane = me // 4
    planes = count // 4
    partner = me + 1 - 2 * core
    across = me + 2 - 4 * side
    ahead = me + 4
    behind = me - 4
    has_ahead = plane + 1 < planes
    has_behind = plane >= 1

    def block(slot):
        return own_ref if slot == 0 else recv.at[slot]

    def chunk(piece):
        if piece == 0:
            return pl.ds(0, SEG_ROWS + rows)
        return pl.ds(SEG_ROWS + piece * rows, rows)

    barrier = pltpu.get_barrier_semaphore()

    def greet(device):
        pl.semaphore_signal(
            barrier, inc=1, device_id={"seq": device}, device_id_type=pl.DeviceIdType.MESH
        )

    greet(partner)
    greet(across)

    @pl.when(has_ahead)
    def _():
        greet(ahead)

    @pl.when(has_behind)
    def _():
        greet(behind)

    both = has_ahead & has_behind
    one = (has_ahead | has_behind) & jnp.logical_not(both)
    neither = jnp.logical_not(has_ahead | has_behind)
    for extra, condition in ((2, both), (1, one), (0, neither)):

        @pl.when(condition)
        def _():
            pl.semaphore_wait(barrier, 2 + extra)

    sent = []

    def copy(kind, piece, source, distance, device):
        src = own_ref if source is None else recv.at[source]
        return pltpu.make_async_remote_copy(
            src_ref=src.at[chunk(piece)],
            dst_ref=recv.at[distance, chunk(piece)],
            send_sem=send_sems.at[kind, piece],
            recv_sem=recv_sems.at[distance, piece],
            device_id={"seq": device},
            device_id_type=pl.DeviceIdType.MESH,
        )

    def send(condition, *what):
        @pl.when(condition)
        def _():
            copy(*what).start()

        sent.append((condition, what))

    def arrive(condition, distance, piece):
        @pl.when(condition)
        def _():
            copy(0, piece, None, distance, partner).wait_recv()

    to_partner = 1 - 2 * core
    has_two = (side == 1) | (plane >= 1)
    has_six = ((side == 1) & (plane >= 1)) | (plane >= 2)
    relays = (side == 1) | (core == 1)
    has_eight = (plane >= 2) & relays
    for piece in range(PIECES):
        send(has_ahead, 0, piece, None, 4, ahead)
        send(side == 0, 1, piece, None, 2, across)
        send(core == 0, 2, piece, None, 1, partner)

    def near(point):
        if point < PIECES:
            arrive(has_behind, 4, point)
            send(has_behind, 3, point, 4, 6 - 4 * side, across)
            send(has_behind & has_ahead & relays, 4, point, 4, 8, ahead)
            send(has_behind, 5, point, 4, 4 + to_partner, partner)
        if point > 0:
            arrive(has_two, 2, point - 1)
            send(has_two, 6, point - 1, 2, 2 + to_partner, partner)

    def far(point):
        if point < PIECES:
            arrive(has_eight, 8, point)
            send(has_eight & (side == 1), 7, point, 8, 6, across)
            send(has_eight & (core == 1), 8, point, 8, 7, partner)
        if point > 0:
            arrive(has_six, 6, point - 1)
            send(has_six, 9, point - 1, 6, 6 + to_partner, partner)

    filler = jnp.full((SEG_ROWS, 2 * HD), NO_SEGMENT, jnp.bfloat16)
    for distance in range(1, SPAN + 1):

        @pl.when(me < distance)
        def _():
            recv[distance, :SEG_ROWS, :] = filler
            recv[distance, SEG_ROWS:, :] = jnp.zeros((kv_heads * rows, 2 * HD), jnp.bfloat16)

    scale = HD ** (-0.5) * 1.4426950408889634
    cosine = cos_ref[...] * scale
    sine = sin_ref[...] * scale

    def turn(head, carry):
        columns = pl.ds(pl.multiple_of(head * HD, HD), HD)
        x = q_ref[:, columns].astype(jnp.float32)
        qa[head] = (x * cosine + pltpu.roll(x, HD // 2, 1) * sine).astype(jnp.bfloat16)
        return carry

    lax.fori_loop(0, heads, turn, 0)

    def segment_row(slot):
        return block(slot)[:SEG_ROWS, :].astype(jnp.float32)[:1]

    qhot[...] = ((one_hot(segment_row(0)) - 1.0) * BIG).astype(jnp.bfloat16)
    key_at = lax.broadcasted_iota(jnp.int32, (rows, rows), 0)
    query_at = lax.broadcasted_iota(jnp.int32, (rows, rows), 1)
    causal[...] = jnp.where(key_at <= query_at, 0.0, -BIG)

    def prepare(slots):
        for slot in slots:
            khot[slot] = one_hot(segment_row(slot)).astype(jnp.bfloat16)

            def flip(kv, carry):
                at = pl.ds(pl.multiple_of(SEG_ROWS + kv * rows, SEG_ROWS), rows)
                flipped = block(slot)[at, HD:].astype(jnp.float32).T
                vt[slot, kv, :HD, :] = flipped.astype(jnp.bfloat16)
                vt[slot, kv, HD:, :] = jnp.ones((ONES_ROWS, rows), jnp.bfloat16)
                return carry

            lax.fori_loop(0, kv_heads, flip, 0)

    def attend(slots, low, high, first, last):
        def step(index, carry):
            for head in (2 * index, 2 * index + 1):
                new_top, mixed = attend_phase(
                    slots, head, group, qa, qhot, block, khot, vt, top, acc,
                    causal if first else None,
                )
                if last:
                    columns = pl.ds(pl.multiple_of(head * HD, HD), HD)
                    result = mixed[:HD] * (1.0 / mixed[HD : HD + 1])
                    out_ref[:, columns] = result.T.astype(jnp.bfloat16)
                else:
                    top[head] = new_top
                    acc[head] = mixed
            return carry

        lax.fori_loop(low // 2, high // 2, step, 0)

    part = heads // PIECES
    prepare((0,))
    for piece in range(PIECES):
        near(piece)
        attend((0,), piece * part, (piece + 1) * part, True, False)
    near(PIECES)
    for piece in range(PIECES):
        arrive(me >= 1, 1, piece)
        arrive(me >= 3, 3, piece)
    prepare((1, 2, 3, 4))
    for piece in range(PIECES):
        far(piece)
        attend((1, 2, 3, 4), piece * part, (piece + 1) * part, False, False)
    far(PIECES)
    for piece in range(PIECES):
        arrive(me >= 5, 5, piece)
        arrive(me >= 7, 7, piece)
    prepare((5, 6, 7))
    attend((5, 6, 7), 0, heads, False, True)

    mine = segment_row(0)
    lead = mine[:, :1]
    earlier = jnp.zeros((1, 1), jnp.float32)
    for distance in range(1, SPAN + 1):
        same = jnp.where(segment_row(distance) == lead, 1.0, 0.0)
        earlier = earlier + jnp.sum(same, axis=1, keepdims=True)
    column = jnp.broadcast_to(mine, (LANES, rows)).T[:, :1]
    before = jnp.sum(jnp.where(mine < column, 1.0, 0.0), axis=1, keepdims=True)
    index = lax.broadcasted_iota(jnp.int32, (rows, 1), 0).astype(jnp.float32)
    positions = index - before + jnp.where(column == lead, earlier, 0.0)
    angles = positions * freq_ref[...]
    lane = lax.broadcasted_iota(jnp.int32, (rows, HD), 1)
    cosine = jnp.cos(angles)
    sine = jnp.where(lane < HD // 2, -1.0, 1.0) * jnp.sin(angles)
    for kv in range(kv_heads):
        x = keys_ref[:, kv * HD : (kv + 1) * HD].astype(jnp.float32)
        turned = x * cosine + pltpu.roll(x, HD // 2, 1) * sine
        rot_ref[:, kv * HD : (kv + 1) * HD] = turned.astype(jnp.bfloat16)

    for condition, what in sent:

        @pl.when(condition)
        def _():
            copy(*what).wait_send()


def local(queries, keys, values, segment_ids):
    rows = queries.shape[0]
    heads = queries.shape[1] // HD
    kv_heads = keys.shape[1] // HD
    count = lax.axis_size("seq")
    row_index = lax.axis_index("seq") * rows + jnp.arange(rows, dtype=jnp.int32)
    cosine, sine = tables(row_index)
    turned = rotate_heads(keys, cosine, sine)
    segment_rows = jnp.broadcast_to(segment_ids.astype(jnp.bfloat16)[None], (SEG_ROWS, rows))
    pieces = [segment_rows]
    for kv in range(kv_heads):
        part = slice(kv * HD, (kv + 1) * HD)
        pieces.append(jnp.concatenate([turned[:, part], values[:, part]], axis=1))
    own = jnp.concatenate(pieces, axis=0)
    inverse_freq = ROPE_BASE ** (-(jnp.arange(HD // 2, dtype=jnp.float32) * (2.0 / HD)))
    frequencies = jnp.concatenate([inverse_freq, inverse_freq])[None]
    vmem = pl.BlockSpec(memory_space=pltpu.VMEM)
    slots = SPAN + 2
    return pl.pallas_call(
        partial(kernel, heads // kv_heads, count),
        out_shape=(
            jax.ShapeDtypeStruct(queries.shape, jnp.bfloat16),
            jax.ShapeDtypeStruct(keys.shape, jnp.bfloat16),
        ),
        in_specs=[vmem] * 6,
        out_specs=(vmem, vmem),
        scratch_shapes=[
            pltpu.VMEM((slots, *own.shape), jnp.bfloat16),
            pltpu.VMEM((heads, rows, HD), jnp.bfloat16),
            pltpu.VMEM((rows, LANES), jnp.bfloat16),
            pltpu.VMEM((slots, rows, LANES), jnp.bfloat16),
            pltpu.VMEM((slots, kv_heads, HD + ONES_ROWS, rows), jnp.bfloat16),
            pltpu.VMEM((heads, 1, rows), jnp.float32),
            pltpu.VMEM((heads, HD + ONES_ROWS, rows), jnp.float32),
            pltpu.VMEM((rows, rows), jnp.float32),
            pltpu.SemaphoreType.DMA((10, PIECES)),
            pltpu.SemaphoreType.DMA((slots, PIECES)),
        ],
        compiler_params=pltpu.CompilerParams(
            vmem_limit_bytes=60 * 1024 * 1024, collective_id=0, has_side_effects=True
        ),
    )(queries, cosine, sine, own, keys, frequencies)


def solution(mesh):
    in_specs = (
        P(("groups", "seq"), None),
        P(("groups", "seq"), None),
        P(("groups", "seq"), None),
        P(("groups", "seq")),
    )
    out_specs = (P(("groups", "seq"), None), P(("groups", "seq"), None))
    return jax.shard_map(local, mesh=mesh, in_specs=in_specs, out_specs=out_specs, check_vma=False)
```

time: 167 us -> 84.3 us (0.50)
  the two profiles are of different devices: /device:TPU:29 before, /device:TPU:24 now
where the time goes in v1:
time: 84.3 us; the launch traced here: 84.1 us
  Pallas kernels  74.4 us (88%)
  local copies, waits for them, and re-layouts  6.29 us (7%)
  other arithmetic  2.59 us (3%)
    pallas_call x1, Pallas kernels, local(): pl.pallas_call(partial(kernel, heads // kv_heads, count), out_shape=(jax....  74.4 us
    unnamed x13, local copies, waits for them, and re-layouts  4.69 us

profile of v1, /device:TPU:24, one launch (start us, length us, event | category | flops | bytes accessed | tf_op | source)
XLA Modules:
  0.0 84.1 jit_solution(792085076335961812)
XLA Ops:
  0.6 0.0 copy-start
  0.7 0.6 maximum_bitcast_fusion.freq_ref
  1.3 0.7 convert_element_type.17
  2.0 1.0 %fusion.4 = (bf16[256,128]{1,0:T(8,128)(2,1)S(1)}, bf16[256,128]{1,0:T(8,128)(2,1)S(1)}, bf16[256,128]{1,0:T(8,128)(2,1)S(1)}, bf16[256,128]{1,0:T(8,128)(2,1)S(1)}) fusion(bf16[256,512]{1,0:T(8,128)(2,1)} %param.6), kind=kLoop, calls=%fused_computation.19 | loop fusion | bytes 524288 | tf_op jit(solution)/shard_map/slice | solution.py:299
  3.0 0.5 fusion.1
  3.5 0.1 pad_maximum_fusion
  3.6 0.0 copy-start.1
  3.7 0.0 copy-start.2
  3.7 0.1 mul.56
  3.8 0.0 copy-done
  3.8 0.2 reshape.26
  3.9 0.3 fusion.2
  4.3 0.4 maximum_multiply_fusion
  4.6 0.0 copy-done.1
  4.7 0.0 copy-done.2
  4.7 0.1 fusion
  5.0 0.0 copy-start.3
  5.0 0.8 copy-done.3
  5.8 74.4 %shard_map.59 = (bf16[256,4096]{1,0:T(8,128)(2,1)}, bf16[256,512]{1,0:T(8,128)(2,1)}) custom-call(bf16[256,4096]{1,0:T(8,128)(2,1)} %q_ref.1, f32[256,128]{1,0:T(8,128)} %copy-done.1, f32[256,128]{1,0:T(8,128)} %copy-done.2, bf16[1040,256]{1,0:T(8,128)(2,1)} %copy-done.3, bf16[256,512]{1,0:T(8,128)(2,1)} %keys_ref.1, f32[1,128]{1,0:T(1,128)} %maximum_bitcast_fusion.freq_ref), custom_call_target="tpu_custom_call" | custom-call | tf_op jit(solution)/shard_map/pallas_call | solution.py:305
  80.2 0.0 copy-start.4
  80.2 3.2 %copy.16 = bf16[256,4096]{1,0:T(8,128)(2,1)} copy(bf16[256,4096]{1,0:T(8,128)(2,1)} %get-tuple-element.19) | data formatting | bytes 4194304
  83.4 0.0 copy-done.4
  83.4 0.7 copy.17
  (8 shorter events, 0.1 us)
Async XLA Ops:
  0.6 3.1 %copy-start = (bf16[256,512]{1,0:T(8,128)(2,1)S(1)}, bf16[256,512]{1,0:T(8,128)(2,1)}, u32[]{:S(2)}) copy-start(bf16[256,512]{1,0:T(8,128)(2,1)} %keys_ref.1) | copy-start | bytes 786436
  3.6 1.0 %copy-start.1 = (f32[256,128]{1,0:T(8,128)}, f32[256,128]{1,0:T(8,128)S(1)}, u32[]{:S(2)}) copy-start(f32[256,128]{1,0:T(8,128)S(1)} %get-tuple-element.15.cos_ref) | copy-start | bytes 393220
  3.7 1.0 %copy-start.2 = (f32[256,128]{1,0:T(8,128)}, f32[256,128]{1,0:T(8,128)S(1)}, u32[]{:S(2)}) copy-start(f32[256,128]{1,0:T(8,128)S(1)} %get-tuple-element.16.sin_ref) | copy-start | bytes 393220
  5.0 0.8 copy-start.3
  80.2 3.2 %copy-start.4 = (bf16[256,512]{1,0:T(8,128)(2,1)S(1)}, bf16[256,512]{1,0:T(8,128)(2,1)}, u32[]{:S(2)}) copy-start(bf16[256,512]{1,0:T(8,128)(2,1)} %get-tuple-element.20) | copy-start | bytes 786436

commit v2 on v1

--- a/solution.py
+++ b/solution.py
@@ -48,24 +48,21 @@
     query = jnp.concatenate([qa[head], qhot[...]], axis=1)
     kv = head // group
     at = pl.ds(pl.multiple_of(SEG_ROWS + kv * rows, SEG_ROWS), rows)
-    parts = []
-    for slot in slots:
-        key = jnp.concatenate([block(slot)[at, :HD], khot[slot]], axis=1)
-        part = lax.dot_general(
-            key, query, (((1,), (1,)), ((), ())), preferred_element_type=jnp.float32
-        )
-        parts.append(part + causal[...] if first else part)
-    new_top = jnp.max(parts[0], axis=0, keepdims=True)
-    for part in parts[1:]:
-        new_top = jnp.maximum(new_top, jnp.max(part, axis=0, keepdims=True))
+    keys = jnp.concatenate(
+        [jnp.concatenate([block(slot)[at, :HD], khot[slot]], axis=1) for slot in slots], axis=0
+    )
+    scores = lax.dot_general(
+        keys, query, (((1,), (1,)), ((), ())), preferred_element_type=jnp.float32
+    )
+    if first:
+        scores = scores + causal[...]
+    new_top = jnp.max(scores, axis=0, keepdims=True)
     if not first:
         old_top = top[head]
         new_top = jnp.maximum(new_top, old_top)
-    mixed = None
-    for slot, part in zip(slots, parts):
-        weights = jnp.exp2(part - new_top).astype(jnp.bfloat16)
-        term = jnp.dot(vt[slot, kv], weights, preferred_element_type=jnp.float32)
-        mixed = term if mixed is None else mixed + term
+    weights = jnp.exp2(scores - new_top).astype(jnp.bfloat16)
+    flipped = vt[kv, :, slots[0] * rows : (slots[-1] + 1) * rows]
+    mixed = jnp.dot(flipped, weights, preferred_element_type=jnp.float32)
     if not first:
         mixed = mixed + acc[head] * jnp.exp2(old_top - new_top)
     return new_top, mixed
@@ -214,8 +211,9 @@
             def flip(kv, carry):
                 at = pl.ds(pl.multiple_of(SEG_ROWS + kv * rows, SEG_ROWS), rows)
                 flipped = block(slot)[at, HD:].astype(jnp.float32).T
-                vt[slot, kv, :HD, :] = flipped.astype(jnp.bfloat16)
-                vt[slot, kv, HD:, :] = jnp.ones((ONES_ROWS, rows), jnp.bfloat16)
+                span = slice(slot * rows, (slot + 1) * rows)
+                vt[kv, :HD, span] = flipped.astype(jnp.bfloat16)
+                vt[kv, HD:, span] = jnp.ones((ONES_ROWS, rows), jnp.bfloat16)
                 return carry
 
             lax.fori_loop(0, kv_heads, flip, 0)
@@ -315,7 +313,7 @@
             pltpu.VMEM((heads, rows, HD), jnp.bfloat16),
             pltpu.VMEM((rows, LANES), jnp.bfloat16),
             pltpu.VMEM((slots, rows, LANES), jnp.bfloat16),
-            pltpu.VMEM((slots, kv_heads, HD + ONES_ROWS, rows), jnp.bfloat16),
+            pltpu.VMEM((kv_heads, HD + ONES_ROWS, slots * rows), jnp.bfloat16),
             pltpu.VMEM((heads, 1, rows), jnp.float32),
             pltpu.VMEM((heads, HD + ONES_ROWS, rows), jnp.float32),
             pltpu.VMEM((rows, rows), jnp.float32),

time: 84.3 us -> 90.4 us (1.072)
  Pallas kernels: 74.4 us -> 80.5 us
    pallas_call x1, Pallas kernels: 74.4 us -> 80.5 us  [local(): pl.pallas_call(partial(kernel, heads // kv_heads, count), out_shape=(jax....]
where the time goes in v2:
time: 90.4 us; the launch traced here: 90.2 us
  Pallas kernels  80.5 us (89%)
  local copies, waits for them, and re-layouts  6.29 us (7%)
  other arithmetic  2.59 us (3%)
    pallas_call x1, Pallas kernels, local(): pl.pallas_call(partial(kernel, heads // kv_heads, count), out_shape=(jax....  80.5 us
    unnamed x13, local copies, waits for them, and re-layouts  4.69 us

profile of v2, /device:TPU:24, one launch (start us, length us, event | category | flops | bytes accessed | tf_op | source)
XLA Modules:
  0.0 90.2 jit_solution(11794123931873507943)
XLA Ops:
  0.6 0.0 copy-start
  0.7 0.6 maximum_bitcast_fusion.freq_ref
  1.3 0.7 convert_element_type.17
  2.0 1.0 %fusion.4 = (bf16[256,128]{1,0:T(8,128)(2,1)S(1)}, bf16[256,128]{1,0:T(8,128)(2,1)S(1)}, bf16[256,128]{1,0:T(8,128)(2,1)S(1)}, bf16[256,128]{1,0:T(8,128)(2,1)S(1)}) fusion(bf16[256,512]{1,0:T(8,128)(2,1)} %param.6), kind=kLoop, calls=%fused_computation.19 | loop fusion | bytes 524288 | tf_op jit(solution)/shard_map/slice | solution.py:297
  3.0 0.5 fusion.1
  3.5 0.1 pad_maximum_fusion
  3.6 0.0 copy-start.1
  3.7 0.0 copy-start.2
  3.7 0.1 mul.56
  3.8 0.0 copy-done
  3.8 0.2 reshape.26
  3.9 0.3 fusion.2
  4.3 0.4 maximum_multiply_fusion
  4.6 0.0 copy-done.1
  4.7 0.0 copy-done.2
  4.7 0.1 fusion
  5.0 0.0 copy-start.3
  5.0 0.8 copy-done.3
  5.8 80.5 %shard_map.59 = (bf16[256,4096]{1,0:T(8,128)(2,1)}, bf16[256,512]{1,0:T(8,128)(2,1)}) custom-call(bf16[256,4096]{1,0:T(8,128)(2,1)} %q_ref.1, f32[256,128]{1,0:T(8,128)} %copy-done.1, f32[256,128]{1,0:T(8,128)} %copy-done.2, bf16[1040,256]{1,0:T(8,128)(2,1)} %copy-done.3, bf16[256,512]{1,0:T(8,128)(2,1)} %keys_ref.1, f32[1,128]{1,0:T(1,128)} %maximum_bitcast_fusion.freq_ref), custom_call_target="tpu_custom_call" | custom-call | tf_op jit(solution)/shard_map/pallas_call | solution.py:303
  86.3 0.0 copy-start.4
  86.3 3.2 %copy.16 = bf16[256,4096]{1,0:T(8,128)(2,1)} copy(bf16[256,4096]{1,0:T(8,128)(2,1)} %get-tuple-element.19) | data formatting | bytes 4194304
  89.5 0.0 copy-done.4
  89.5 0.7 copy.17
  (8 shorter events, 0.1 us)
Async XLA Ops:
  0.6 3.1 %copy-start = (bf16[256,512]{1,0:T(8,128)(2,1)S(1)}, bf16[256,512]{1,0:T(8,128)(2,1)}, u32[]{:S(2)}) copy-start(bf16[256,512]{1,0:T(8,128)(2,1)} %keys_ref.1) | copy-start | bytes 786436
  3.6 1.0 %copy-start.1 = (f32[256,128]{1,0:T(8,128)}, f32[256,128]{1,0:T(8,128)S(1)}, u32[]{:S(2)}) copy-start(f32[256,128]{1,0:T(8,128)S(1)} %get-tuple-element.15.cos_ref) | copy-start | bytes 393220
  3.7 1.0 %copy-start.2 = (f32[256,128]{1,0:T(8,128)}, f32[256,128]{1,0:T(8,128)S(1)}, u32[]{:S(2)}) copy-start(f32[256,128]{1,0:T(8,128)S(1)} %get-tuple-element.16.sin_ref) | copy-start | bytes 393220
  5.0 0.8 copy-start.3
  86.3 3.2 %copy-start.4 = (bf16[256,512]{1,0:T(8,128)(2,1)S(1)}, bf16[256,512]{1,0:T(8,128)(2,1)}, u32[]{:S(2)}) copy-start(bf16[256,512]{1,0:T(8,128)(2,1)} %get-tuple-element.20) | copy-start | bytes 786436
